TPU v7x, 32 devices: a whole 2x2x4 slice. The times are simulated.
32 devices in a mesh: seq: 4 (over y, core), tp: 8 (over z, x).
Axes of the slice: x: 2, y: 2, z: 4, core: 2. Of those that a mesh axis runs over, the one named last changes fastest.
Arguments:
- tokens: bfloat16 [2048, 4608], P(('seq', 'tp')), may hold values from -6 to 6
- norm_gain: float32 [4608], replicated, may hold values from 0.1 to 1.9
- query_weight: bfloat16 [4608, 4096], P(None, 'tp'), may hold values from -6 to 6
- key_matrix: bfloat16 [4608, 2048], P(None, 'tp'), may hold values from -0.09375 to 0.09375
- value_matrix: bfloat16 [4608, 2048], P(None, 'tp'), may hold values from -0.09375 to 0.09375
- output_grad: bfloat16 [2048, 4096], P('seq', 'tp'), may hold values from -3 to 3
Outputs:
- input_gradient: bfloat16 [2048, 4608], P(('seq', 'tp'))
All inputs are finite; a program needn't handle non-finite values.
Results may differ from a plain program's by a relative error of at most 0.014.
The roundings to bfloat16 on the way count: a program that leaves them out, or rounds other values in their place, can miss the bound.
Values may be sent and summed in bfloat16 or wider, within the bound.
A program may use at most 64 MiB of HBM per device.

v0:
```python
import jax
import jax.numpy as jnp
from jax import lax
from jax.sharding import PartitionSpec as P

HEAD_SIZE = 128
WINDOW = 640


SCALE = 1.0 / 12.0
CAP = 50.0
EPS = 1e-06


def shifted(block, axis, distance):
    devices = range(lax.axis_size(axis))
    route = [(i - distance, i) for i in devices if i - distance in devices]
    return lax.ppermute(block, axis, route)


def normalize_project(rows_piece, norm_gain, query_weight, key_matrix, value_matrix):
    float_values = rows_piece.astype(jnp.float32)
    reciprocal_norm = lax.rsqrt(jnp.mean(float_values * float_values, axis=1, keepdims=True) + EPS)
    normed = (float_values * reciprocal_norm * norm_gain).astype(jnp.bfloat16)
    outputs = [
        jnp.dot(normed, weight, preferred_element_type=jnp.float32).astype(jnp.bfloat16)
        for weight in (query_weight, key_matrix, value_matrix)
    ]
    return jnp.concatenate(outputs, axis=1)


def block_grads(query_blk, grad_blk, key_blk, value_blk, query_pos, key_pos):
    row_count = query_blk.shape[0]
    key_span = key_blk.shape[0]
    kv_heads = key_blk.shape[1] // HEAD_SIZE
    groups = query_blk.shape[1] // key_blk.shape[1]
    query_four = query_blk.reshape(row_count, kv_heads, groups, HEAD_SIZE)
    grad_four = grad_blk.reshape(row_count, kv_heads, groups, HEAD_SIZE)
    key_three = key_blk.reshape(key_span, kv_heads, HEAD_SIZE)
    value_three = value_blk.reshape(key_span, kv_heads, HEAD_SIZE)
    raw = jnp.einsum("qkgd,skd->kgqs", query_four, key_three, preferred_element_type=jnp.float32)
    bent = jnp.tanh(raw * SCALE / CAP)
    capped = CAP * bent
    valid = (
        (key_pos[None, :] <= query_pos[:, None])
        & (key_pos[None, :] > query_pos[:, None] - WINDOW)
        & (key_pos[None, :] >= 0)
    )
    expo = jnp.where(valid, jnp.exp(capped), 0.0)
    probs = expo / jnp.sum(expo, axis=-1, keepdims=True)
    d_probs = jnp.einsum(
        "qkgd,skd->kgqs", grad_four, value_three, preferred_element_type=jnp.float32
    )
    delta = jnp.sum(probs * d_probs, axis=-1, keepdims=True)
    d_raw = (probs * (d_probs - delta) * (1.0 - bent * bent) * SCALE).astype(jnp.bfloat16)
    probs_low = probs.astype(jnp.bfloat16)
    grad_query = jnp.einsum(
        "kgqs,skd->qkgd", d_raw, key_three, preferred_element_type=jnp.float32
    ).reshape(row_count, kv_heads * groups * HEAD_SIZE)
    grad_key = jnp.einsum(
        "kgqs,qkgd->skd", d_raw, query_four, preferred_element_type=jnp.float32
    ).reshape(key_span, kv_heads * HEAD_SIZE)
    grad_value = jnp.einsum(
        "kgqs,qkgd->skd", probs_low, grad_four, preferred_element_type=jnp.float32
    ).reshape(key_span, kv_heads * HEAD_SIZE)
    return (grad_query, grad_key, grad_value)


def row_product(grad_rows, weight):
    return lax.dot_general(
        grad_rows, weight, (((1,), (1,)), ((), ())), preferred_element_type=jnp.float32
    )


def on_device(tokens, norm_gain, query_weight, key_matrix, value_matrix, output_grad):
    local_rows = output_grad.shape[0]
    query_cols = query_weight.shape[1]
    key_cols = key_matrix.shape[1]
    reach = WINDOW - local_rows
    block_rows = min(512, local_rows)
    key_span = WINDOW + block_rows
    joined = normalize_project(
        lax.all_gather(tokens, "tp", axis=0, tiled=True),
        norm_gain,
        query_weight,
        key_matrix,
        value_matrix,
    )
    query_own = joined[:, :query_cols]
    key_own = joined[:, query_cols : query_cols + key_cols]
    value_own = joined[:, query_cols + key_cols :]
    near_key, near_value = shifted((key_own, value_own), "seq", 1)
    far_key, far_value = shifted(
        (key_own[local_rows - reach :], value_own[local_rows - reach :]), "seq", 2
    )
    all_key = jnp.concatenate([far_key, near_key, key_own], axis=0)
    all_value = jnp.concatenate([far_value, near_value, value_own], axis=0)
    anchor = lax.axis_index("seq") * local_rows
    acc_key = jnp.zeros((WINDOW + local_rows, key_cols), jnp.float32)
    acc_value = jnp.zeros((WINDOW + local_rows, key_cols), jnp.float32)
    query_pos = anchor + 0 + jnp.arange(block_rows, dtype=jnp.int32)
    key_pos = anchor + 0 - WINDOW + jnp.arange(key_span, dtype=jnp.int32)
    grad_query, grad_key, grad_value = block_grads(
        query_own, output_grad, all_key, all_value, query_pos, key_pos
    )
    acc_key = acc_key.at[0:key_span].add(grad_key)
    acc_value = acc_value.at[0:key_span].add(grad_value)
    query_grads = grad_query.astype(jnp.bfloat16)
    far_gkey = acc_key[:reach]
    far_gvalue = acc_value[:reach]
    near_gkey = acc_key[reach : reach + local_rows]
    near_gvalue = acc_value[reach : reach + local_rows]
    own_gkey = acc_key[reach + local_rows :]
    own_gvalue = acc_value[reach + local_rows :]
    far_back_key, far_back_value = shifted((far_gkey, far_gvalue), "seq", -2)
    back_key, back_value = shifted((near_gkey, near_gvalue), "seq", -1)
    own_gkey = own_gkey + back_key
    own_gvalue = own_gvalue + back_value
    own_gkey = own_gkey.at[local_rows - reach :].add(far_back_key)
    own_gvalue = own_gvalue.at[local_rows - reach :].add(far_back_value)
    key_low = own_gkey.astype(jnp.bfloat16)
    value_low = own_gvalue.astype(jnp.bfloat16)
    total_term = row_product(query_grads, query_weight)
    total_term = total_term + row_product(key_low, key_matrix)
    d_norm = lax.psum_scatter(
        total_term + row_product(value_low, value_matrix), "tp", scatter_dimension=0, tiled=True
    )
    float_values = tokens.astype(jnp.float32)
    reciprocal_norm = lax.rsqrt(jnp.mean(float_values * float_values, axis=1, keepdims=True) + EPS)
    upper_limit = d_norm * norm_gain
    normalized_input = float_values * reciprocal_norm
    input_gradient = reciprocal_norm * (
        upper_limit
        - normalized_input * jnp.mean(upper_limit * normalized_input, axis=1, keepdims=True)
    )
    return input_gradient.astype(jnp.bfloat16)


def solution(mesh):
    return jax.shard_map(
        on_device,
        mesh=mesh,
        in_specs=(
            P(("seq", "tp"), None),
            P(),
            P(None, "tp"),
            P(None, "tp"),
            P(None, "tp"),
            P("seq", "tp"),
        ),
        out_specs=P(("seq", "tp"), None),
        check_vma=False,
    )
```

profile of v0, /device:TPU:0, one launch (start us, length us, event | category | flops | bytes accessed | tf_op | source)
XLA Modules:
  0.0 376.6 jit_solution(9653311893669819124)
XLA Ops:
  7.3 2.1 copy.31
  9.4 1.6 and_and_fusion
  11.1 80.5 %all-gather.2.cloned.1.call-done = bf16[512,4608]{1,0:T(8,128)(2,1)} async-done(((bf16[64,4608]{1,0:T(8,128)(2,1)}), bf16[512,4608]{1,0:T(8,128)(2,1)}) %all-gather.2.cloned.1.call-update) | async-done | bytes 4718608 | tf_op jit(solution)/shard_map/all_gather | solution.py:83
  91.6 3.5 fusion.1
  95.1 3.8 %convolution_convert_fusion.2 = bf16[512,256]{1,0:T(8,128)(2,1)S(1)} fusion(bf16[4608,256]{1,0:T(8,128)(2,1)S(1)} %copy-done, bf16[512,4608]{1,0:T(8,128)(2,1)} %all-gather.2.cloned.1.call-done, f32[4608]{0:T(1024)} %param.19, f32[512]{0:T(512)S(1)} %add_rsqrt_fusion), kind=kOutput, calls=%fused_computation.31 | convolution fusion | flops 1217527808 | bytes 7360512 | tf_op jit(solution)/shard_map/dot_general | solution.py:26
  99.0 1.6 collective-permute-start.1
  100.6 2.2 convolution_convert_fusion.1
  102.8 1.5 slice.125
  104.3 4.8 %collective-permute-start.3 = (bf16[512,256]{1,0:T(8,128)(2,1)}, bf16[512,256]{1,0:T(8,128)(2,1)}, u32[]{:S(2)}, u32[]{:S(2)}) collective-permute-start(bf16[512,256]{1,0:T(8,128)(2,1)} %convolution_convert_fusion.1), channel_id=1, source_target_pairs={{0,8},{8,16},{16,24},{1,9},{9,17},{17,25},{2,10},{10,18},{18,26},{... | collective-permute-start | bytes 786440 | tf_op jit(solution)/shard_map/ppermute | solution.py:18
  109.0 1.9 collective-permute-start.2
  111.0 1.5 collective-permute-start
  112.5 3.5 convolution_convert_fusion
  116.2 1.7 copy.19
  119.1 6.2 %fusion.24 = f32[2,1152,512,2]{2,1,3,0:T(8,128)} fusion(bf16[512,2,2,128]{0,3,2,1:T(8,128)(2,1)} %bitcast.104, bf16[1152,2,128,1]{2,1,0,3:T(2,128)(2,1)S(1)} %bitcast.102), kind=kOutput, calls=%fused_computation.39 | convolution fusion | flops 603979776 | bytes 10551296 | tf_op jit(solution)/shard_map/qkgd,skd->kgqs/dot_general | solution.py:51
  125.3 5.5 %fusion.8 = (f32[2,2,512]{2,1,0:T(2,128)S(1)}, f32[2,1152,512,2]{2,1,3,0:T(8,128)}) fusion(pred[512,1152]{0,1:T(8,128)(4,1)S(1)} %copy-done.6, bf16[1152,2,128,1]{0,2,3,1:T(8,128)(2,1)S(1)} %copy-done.7, bf16[512,2,2,128]{0,3,2,1:T(8,128)(2,1)S(1)} %bitcast.112), kind=kOutput, calls=%fused_computation.16 | convolution fusion | flops 613414912 | bytes 11149312 | tf_op jit(solution)/shard_map/qkgd,skd->kgqs/dot_general | solution.py:41
  130.9 16.9 %fusion.18 = bf16[2,128,2,512]{3,1,2,0:T(8,128)(2,1)} fusion(bf16[1152,2,128,1]{0,2,3,1:T(8,128)(2,1)S(1)} %copy-done.8, f32[2,1152,512,2]{2,1,3,0:T(8,128)} %fusion.24, f32[2,1152,512,2]{2,1,3,0:T(8,128)} %get-tuple-element.74, f32[2,2,512]{2,1,0:T(2,128)S(1)} %get-tuple-element.73, pred[512,1152]{0,1:T(8,128)(4,1)S(1)} %copy-done.6), kind=kOutput, calls=%fused_computation.28 | convolution fusion | flops 641993856 | bytes 20586496 | tf_op jit(solution)/shard_map/kgqs,skd->qkgd/dot_general | solution.py:57
  147.7 22.3 %convolution_bitcast_fusion = f32[1152,2,128]{0,2,1:T(8,128)} fusion(bf16[512,2,2,128]{0,3,2,1:T(8,128)(2,1)} %bitcast.111, f32[2,1152,512,2]{2,1,3,0:T(8,128)} %fusion.24, f32[2,1152,512,2]{2,1,3,0:T(8,128)} %get-tuple-element.74, f32[2,2,512]{2,1,0:T(2,128)S(1)} %get-tuple-element.73, pred[512,1152]{0,1:T(8,128)(4,1)S(1)} %copy-done.6), kind=kOutput, calls=%fused_computation.21 | convolution fusion | flops 641731712 | bytes 21176320 | tf_op jit(solution)/shard_map/kgqs,qkgd->skd/dot_general | solution.py:60
  170.0 6.1 %fusion.12 = f32[1152,2,128]{0,2,1:T(8,128)S(1)} fusion(bf16[512,2,2,128]{0,3,2,1:T(8,128)(2,1)S(1)} %bitcast.105, f32[2,1152,512,2]{2,1,3,0:T(8,128)} %get-tuple-element.74, f32[2,2,512]{2,1,0:T(2,128)S(1)} %get-tuple-element.73, pred[512,1152]{0,1:T(8,128)(4,1)S(1)} %copy-done.6), kind=kOutput, calls=%fused_computation.20 | convolution fusion | flops 615776256 | bytes 11739136 | tf_op jit(solution)/shard_map/kgqs,qkgd->skd/dot_general | solution.py:63
  181.7 4.9 %fusion.49 = f32[512,4608]{1,0:T(8,128)S(1)} fusion(bf16[512,512]{0,1:T(8,128)(2,1)S(1)} %bitcast.106, bf16[4608,512]{1,0:T(8,128)(2,1)} %param.20), kind=kOutput, calls=%fused_computation.67 | convolution fusion | flops 2415919104 | bytes 14680064 | tf_op jit(solution)/shard_map/dot_general | solution.py:70
  186.8 5.1 %fusion.27 = f32[512,4608]{1,0:T(8,128)} fusion(bf16[4608,256]{1,0:T(8,128)(2,1)S(1)} %copy-done, f32[512,256]{0,1:T(8,128)S(1)} %fusion.30), kind=kOutput, calls=%fused_computation.44 | convolution fusion | flops 1208090624 | bytes 12320768 | tf_op jit(solution)/shard_map/dot_general | solution.py:70
  192.1 9.2 %add_add_fusion = f32[512,4608]{1,0:T(8,128)} fusion(f32[512,4608]{1,0:T(8,128)S(1)} %fusion.49, f32[512,4608]{1,0:T(8,128)} %fusion.27, bf16[4608,256]{1,0:T(8,128)(2,1)S(1)} %copy-done.3, f32[512,256]{0,1:T(8,128)S(1)} %fusion.29), kind=kOutput, calls=%fused_computation.13 | convolution fusion | flops 1212809216 | bytes 31195136 | tf_op jit(solution)/shard_map/dot_general | solution.py:70
  202.5 163.2 %reduce-scatter.2.cloned.1.call-done = f32[64,4608]{1,0:T(8,128)} async-done(((f32[512,4608]{1,0:T(8,128)}), f32[64,4608]{1,0:T(8,128)}) %reduce-scatter.2.cloned.1.call-update) | async-done | bytes 1179664 | tf_op jit(solution)/shard_map/reduce_scatter | solution.py:125
  365.7 1.6 fusion.19
  367.4 2.4 fusion.22
  (72 shorter events, 9.3 us)
Async XLA Ops:
  6.5 88.6 %copy-start = (bf16[4608,256]{1,0:T(8,128)(2,1)S(1)}, bf16[4608,256]{1,0:T(8,128)(2,1)}, u32[]{:S(2)}) copy-start(bf16[4608,256]{1,0:T(8,128)(2,1)} %param.21) | copy-start | bytes 7077892
  6.5 85.1 %all-gather.2.cloned.1.call-start = ((), (), s32[]{:S(2)}) async-start(), calls=%async_computation.1 | async-start | bytes 5308416 | tf_op jit(solution)/shard_map/all_gather | solution.py:83
  7.3 358.5 %reduce-scatter.2.cloned.1.call-start = ((), (), s32[]{:S(2)}) async-start(), calls=%async_computation.2 | async-start | bytes 10616832 | tf_op jit(solution)/shard_map/reduce_scatter | solution.py:125
  9.4 91.2 %copy-start.10 = (f32[4608]{0:T(1024)S(1)}, f32[4608]{0:T(1024)}, u32[]{:S(2)}) copy-start(f32[4608]{0:T(1024)} %param.19) | copy-start | bytes 55300
  91.6 9.0 %slice-start.2 = ((s8[4718592]{0:T(1024)(128)(4,1)}), s8[4194304]{0:T(1024)(128)(4,1)S(1)}, s32[]{:S(2)}) async-start(s8[4718592]{0:T(1024)(128)(4,1)} %bitcast.100), calls=%async_computation.5 | async-start | bytes 8388608
  91.6 9.0 %copy-start.2 = (bf16[4608,256]{1,0:T(8,128)(2,1)S(1)}, bf16[4608,256]{1,0:T(8,128)(2,1)}, u32[]{:S(2)}) copy-start(bf16[4608,256]{1,0:T(8,128)(2,1)} %param.22) | copy-start | bytes 7077892
  99.0 13.5 %slice-start = ((s8[4718592]{0:T(1024)(128)(4,1)}), s8[4194304]{0:T(1024)(128)(4,1)S(1)}, s32[]{:S(2)}) async-start(s8[4718592]{0:T(1024)(128)(4,1)} %bitcast.98), calls=%async_computation.3 | async-start | bytes 8388608
  99.0 13.5 %slice-start.1 = ((s8[4718592]{0:T(1024)(128)(4,1)}), s8[524288]{0:T(1024)(128)(4,1)S(1)}, s32[]{:S(2)}) async-start(s8[4718592]{0:T(1024)(128)(4,1)} %bitcast.98), calls=%async_computation.4 | async-start | bytes 1048576
  99.0 17.0 %collective-permute-start.1 = (bf16[512,256]{1,0:T(8,128)(2,1)S(1)}, bf16[512,256]{1,0:T(8,128)(2,1)S(1)}, u32[]{:S(2)}, u32[]{:S(2)}) collective-permute-start(bf16[512,256]{1,0:T(8,128)(2,1)S(1)} %convolution_convert_fusion.2), channel_id=1, source_target_pairs={{0,8},{8,16},{16,24},{1,9},{9,17},{17,25},{2,10},{10,18},{18,26},{... | collective-permute-start | bytes 786440 | tf_op jit(solution)/shard_map/ppermute | solution.py:18
  104.3 13.6 %collective-permute-start.3 = (bf16[512,256]{1,0:T(8,128)(2,1)}, bf16[512,256]{1,0:T(8,128)(2,1)}, u32[]{:S(2)}, u32[]{:S(2)}) collective-permute-start(bf16[512,256]{1,0:T(8,128)(2,1)} %convolution_convert_fusion.1), channel_id=1, source_target_pairs={{0,8},{8,16},{16,24},{1,9},{9,17},{17,25},{2,10},{10,18},{18,26},{... | collective-permute-start | bytes 786440 | tf_op jit(solution)/shard_map/ppermute | solution.py:18
  109.0 8.8 %collective-permute-start.2 = (bf16[128,256]{1,0:T(8,128)(2,1)}, bf16[128,256]{1,0:T(8,128)(2,1)}, u32[]{:S(2)}, u32[]{:S(2)}) collective-permute-start(bf16[128,256]{1,0:T(8,128)(2,1)} %slice.125), channel_id=1, source_target_pairs={{0,16},{8,24},{1,17},{9,25},{2,18},{10,26},{3,19},{11,27},{4,20},{... | collective-permute-start | bytes 196616 | tf_op jit(solution)/shard_map/ppermute | solution.py:18
  111.0 5.0 %collective-permute-start = (bf16[128,256]{1,0:T(8,128)(2,1)S(1)}, bf16[128,256]{1,0:T(8,128)(2,1)S(1)}, u32[]{:S(2)}, u32[]{:S(2)}) collective-permute-start(bf16[128,256]{1,0:T(8,128)(2,1)S(1)} %slice.124), channel_id=1, source_target_pairs={{0,16},{8,24},{1,17},{9,25},{2,18},{10,26},{3,19},{11,27},{4,20},{... | collective-permute-start | bytes 196616 | tf_op jit(solution)/shard_map/ppermute | solution.py:18
  119.1 6.2 %copy-start.6 = (pred[512,1152]{0,1:T(8,128)(4,1)S(1)}, pred[512,1152]{0,1:T(8,128)(4,1)}, u32[]{:S(2)}) copy-start(pred[512,1152]{0,1:T(8,128)(4,1)} %and_and_fusion) | copy-start | bytes 1769476
  119.1 6.2 %copy-start.7 = (bf16[1152,2,128,1]{0,2,3,1:T(8,128)(2,1)S(1)}, bf16[1152,2,128,1]{0,2,3,1:T(8,128)(2,1)}, u32[]{:S(2)}) copy-start(bf16[1152,2,128,1]{0,2,3,1:T(8,128)(2,1)} %copy.19) | copy-start | bytes 1769476
  119.1 6.2 %copy-start.12 = (bf16[512,512]{0,1:T(8,128)(2,1)S(1)}, bf16[512,512]{0,1:T(8,128)(2,1)}, u32[]{:S(2)}) copy-start(bf16[512,512]{0,1:T(8,128)(2,1)} %convolution_convert_fusion) | copy-start | bytes 1572868
  125.3 5.5 %copy-start.8 = (bf16[1152,2,128,1]{0,2,3,1:T(8,128)(2,1)S(1)}, bf16[1152,2,128,1]{0,2,3,1:T(8,128)(2,1)}, u32[]{:S(2)}) copy-start(bf16[1152,2,128,1]{0,2,3,1:T(8,128)(2,1)} %copy.19) | copy-start | bytes 1769476
  147.7 22.3 %copy-start.4 = (bf16[512,512]{0,1:T(8,128)(2,1)S(1)}, bf16[512,512]{0,1:T(8,128)(2,1)}, u32[]{:S(2)}) copy-start(bf16[512,512]{0,1:T(8,128)(2,1)} %copy.31) | copy-start | bytes 1572868
  170.0 6.3 %copy-start.5 = (f32[1152,2,128]{0,2,1:T(8,128)S(1)}, f32[1152,2,128]{0,2,1:T(8,128)}, u32[]{:S(2)}) copy-start(f32[1152,2,128]{0,2,1:T(8,128)} %convolution_bitcast_fusion) | copy-start | bytes 3538948
  170.0 11.7 %copy-start.9 = (bf16[2,128,2,512]{3,1,2,0:T(8,128)(2,1)S(1)}, bf16[2,128,2,512]{3,1,2,0:T(8,128)(2,1)}, u32[]{:S(2)}) copy-start(bf16[2,128,2,512]{3,1,2,0:T(8,128)(2,1)} %fusion.18) | copy-start | bytes 1572868
  176.5 10.2 %collective-permute-start.5 = (f32[128,256]{0,1:T(8,128)S(1)}, f32[128,256]{0,1:T(8,128)S(1)}, u32[]{:S(2)}, u32[]{:S(2)}) collective-permute-start(f32[128,256]{0,1:T(8,128)S(1)} %bitcast.110), channel_id=1, source_target_pairs={{16,0},{24,8},{17,1},{25,9},{18,2},{26,10},{19,3},{27,11},{20,4},{... | collective-permute-start | bytes 393224 | tf_op jit(solution)/shard_map/ppermute | solution.py:18
  177.8 14.2 %collective-permute-start.7 = (f32[128,256]{0,1:T(8,128)S(1)}, f32[128,256]{0,1:T(8,128)S(1)}, u32[]{:S(2)}, u32[]{:S(2)}) collective-permute-start(f32[128,256]{0,1:T(8,128)S(1)} %bitcast.109), channel_id=1, source_target_pairs={{16,0},{24,8},{17,1},{25,9},{18,2},{26,10},{19,3},{27,11},{20,4},{... | collective-permute-start | bytes 393224 | tf_op jit(solution)/shard_map/ppermute | solution.py:18
  179.1 7.5 %collective-permute-start.4 = (f32[512,256]{0,1:T(8,128)S(1)}, f32[512,256]{0,1:T(8,128)S(1)}, u32[]{:S(2)}, u32[]{:S(2)}) collective-permute-start(f32[512,256]{0,1:T(8,128)S(1)} %bitcast.108), channel_id=1, source_target_pairs={{8,0},{16,8},{24,16},{9,1},{17,9},{25,17},{10,2},{18,10},{26,18},{... | collective-permute-start | bytes 1572872 | tf_op jit(solution)/shard_map/ppermute | solution.py:18
  180.4 11.5 %collective-permute-start.6 = (f32[512,256]{0,1:T(8,128)S(1)}, f32[512,256]{0,1:T(8,128)S(1)}, u32[]{:S(2)}, u32[]{:S(2)}) collective-permute-start(f32[512,256]{0,1:T(8,128)S(1)} %bitcast.107), channel_id=1, source_target_pairs={{8,0},{16,8},{24,16},{9,1},{17,9},{25,17},{10,2},{18,10},{26,18},{... | collective-permute-start | bytes 1572872 | tf_op jit(solution)/shard_map/ppermute | solution.py:18
  201.2 164.5 %copy-start.11 = (f32[4608]{0:T(1024)S(1)}, f32[4608]{0:T(1024)}, u32[]{:S(2)}) copy-start(f32[4608]{0:T(1024)} %param.19) | copy-start | bytes 55300
  (3 other events, 12.0 us)
Sparse Core Ops, SparseCore 0:
  9.5 82.0 all-gather.1
  201.4 164.2 reduce-scatter.1
where the time goes:
time: 377 us
  waiting for transfers between devices  244 us (65%)
  matrix products  85.7 us (23%)
  starting transfers between devices  14.9 us (4%)
  between operations  13.8 us (4%)
  other arithmetic  10.8 us (3%)
  local copies, waits for them, and re-layouts  6.91 us (2%)
    reduce_scatter x1, waiting for transfers between devices, on_device(): lax.psum_scatter(total_term + row_product(value_low, value_matrix), 'tp',...  163 us
    all_gather x1, waiting for transfers between devices, on_device(): lax.all_gather(tokens, 'tp', axis=0, tiled=True)  80.5 us
    dot_general x1, matrix products, block_grads(): jnp.einsum('kgqs,qkgd->skd', d_raw, query_four, preferred_element_type=jn...  22.3 us
    dot_general x3, matrix products, row_product(): lax.dot_general(grad_rows, weight, (((1,), (1,)), ((), ())), preferred_el...  19.2 us
    dot_general x1, matrix products, block_grads(): jnp.einsum('kgqs,skd->qkgd', d_raw, key_three, preferred_element_type=jnp...  16.9 us
    ppermute x8, starting transfers between devices, shifted(): return lax.ppermute(block, axis, route)  14.9 us
    dot_general x3, matrix products, normalize_project(): jnp.dot(normed, weight, preferred_element_type=jnp.float32)  9.53 us
  transfers between devices with their start and end apart: 10, of which 2 were waited for; matrix products, arithmetic and copies ran while one was open for 6% of the time, Pallas kernels for 0%

commit v1 on v0

v1 whole, which is shorter than its diff:
```python
import functools

import jax
import jax.numpy as jnp
from jax import lax
from jax.experimental import pallas as pl
from jax.experimental.pallas import tpu as pltpu
from jax.sharding import PartitionSpec as P

HEAD_SIZE = 128
WINDOW = 640


SCALE = 1.0 / 12.0
CAP = 50.0
EPS = 1e-06
VMEM_BYTES = 60 * 1024 * 1024


def shifted(block, axis, distance):
    devices = range(lax.axis_size(axis))
    route = [(i - distance, i) for i in devices if i - distance in devices]
    return lax.ppermute(block, axis, route)


def ring_place(index, n):
    odd = index % 2
    return (1 - odd) * (index // 2) + odd * (n - 1 - index // 2)


def ring_device(place, n):
    place = (place + n) % n
    late = place // (n // 2)
    return (1 - late) * 2 * place + late * (2 * (n - 1 - place) + 1)


def chunks_of(direction, hop, last):
    return (direction, 1 - direction) if hop < last else (direction,)


def greet(neighbours):
    barrier = pltpu.get_barrier_semaphore()
    for neighbour in neighbours:
        pl.semaphore_signal(
            barrier, inc=1, device_id={"tp": neighbour}, device_id_type=pl.DeviceIdType.MESH
        )
    pl.semaphore_wait(barrier, 2)


def load_weights(weights, held, sems):
    copies = []
    start = 0
    for i, weight in enumerate(weights):
        cols = weight.shape[1]
        copies.append(
            pltpu.make_async_copy(weight, held.at[:, start : start + cols], sems.at[i])
        )
        start += cols
    for copy in copies:
        copy.start()
    return copies


def gather_kernel(
    n, tokens, gain, wq, wk, wv, out, gathered, held, normed, send_sems, recv_sems, load_sems
):
    rows, width = tokens.shape
    half = rows // 2
    last = n // 2
    cols = out.shape[1]
    tile = 256
    place = ring_place(lax.axis_index("tp"), n)
    ahead = (ring_device(place + 1, n), ring_device(place - 1, n))
    loads = load_weights((wq, wk, wv), held, load_sems)
    greet(ahead)

    def sender(direction, hop, chunk):
        step = -(hop - 1) if direction == 0 else hop - 1
        owner = ring_device(place + step, n)
        part = pl.ds(chunk * half, half)
        source = tokens.at[part] if hop == 1 else gathered.at[owner, part]
        return pltpu.make_async_remote_copy(
            src_ref=source,
            dst_ref=gathered.at[owner, part],
            send_sem=send_sems.at[direction, hop - 1, chunk],
            recv_sem=recv_sems.at[direction, hop - 1, chunk],
            device_id={"tp": ahead[direction]},
            device_id_type=pl.DeviceIdType.MESH,
        )

    def project(sources):
        for i, (block, _) in enumerate(sources):
            values = block[...].astype(jnp.float32)
            scale = lax.rsqrt(jnp.mean(values * values, axis=1, keepdims=True) + EPS)
            normed[i * rows : (i + 1) * rows] = (values * scale * gain[...]).astype(jnp.bfloat16)
        count = len(sources) * rows

        def column(j, carry):
            at = pl.ds(pl.multiple_of(j * tile, tile), tile)
            product = jnp.dot(
                normed[:count], held[:, at], preferred_element_type=jnp.float32
            ).astype(jnp.bfloat16)
            for i, (_, owner) in enumerate(sources):
                out[pl.ds(pl.multiple_of(owner * rows, rows), rows), at] = product[
                    i * rows : (i + 1) * rows
                ]
            return carry

        lax.fori_loop(0, cols // tile, column, 0)

    sends = []
    for position in range(2):
        for direction in range(2):
            order = chunks_of(direction, 1, last)
            if position < len(order):
                sends.append(sender(direction, 1, order[position]))
                sends[-1].start()
    for copy in loads:
        copy.wait()
    project([(tokens, lax.axis_index("tp"))])
    for hop in range(1, last + 1):
        for position in range(2):
            for direction in range(2):
                order = chunks_of(direction, hop, last)
                if position < len(order):
                    chunk = order[position]
                    sender(direction, hop, chunk).wait_recv()
                    if hop < last and chunk in chunks_of(direction, hop + 1, last):
                        sends.append(sender(direction, hop + 1, chunk))
                        sends[-1].start()
        owners = [ring_device(place - hop, n)]
        if hop < last:
            owners.append(ring_device(place + hop, n))
        project([(gathered.at[owner], owner) for owner in owners])
    for copy in sends:
        copy.wait_send()


def gather_project(tokens, norm_gain, weights):
    n = lax.axis_size("tp")
    rows, width = tokens.shape
    cols = sum(weight.shape[1] for weight in weights)
    vmem = pl.BlockSpec(memory_space=pltpu.VMEM)
    hbm = pl.BlockSpec(memory_space=pl.ANY)
    return pl.pallas_call(
        functools.partial(gather_kernel, n),
        out_shape=jax.ShapeDtypeStruct((n * rows, cols), jnp.bfloat16),
        in_specs=[vmem, vmem, hbm, hbm, hbm],
        out_specs=vmem,
        scratch_shapes=[
            pltpu.VMEM((n, rows, width), jnp.bfloat16),
            pltpu.VMEM((width, cols), jnp.bfloat16),
            pltpu.VMEM((2 * rows, width), jnp.bfloat16),
            pltpu.SemaphoreType.DMA((2, n // 2, 2)),
            pltpu.SemaphoreType.DMA((2, n // 2, 2)),
            pltpu.SemaphoreType.DMA((3,)),
        ],
        compiler_params=pltpu.CompilerParams(
            collective_id=0, has_side_effects=True, vmem_limit_bytes=VMEM_BYTES
        ),
        name="gather_project",
    )(tokens, norm_gain.reshape(1, width), *weights)


def scatter_kernel(
    n,
    grads,
    tokens,
    gain,
    wq,
    wk,
    wv,
    out,
    outgoing,
    incoming,
    held,
    picked,
    total,
    send_sems,
    recv_sems,
    load_sems,
):
    rows, width = tokens.shape
    half = rows // 2
    last = n // 2
    tile = 256
    place = ring_place(lax.axis_index("tp"), n)
    ahead = (ring_device(place + 1, n), ring_device(place - 1, n))
    loads = load_weights((wq, wk, wv), held, load_sems)
    greet(ahead)

    def sender(direction, hop, chunk):
        part = pl.ds(chunk * half, half)
        return pltpu.make_async_remote_copy(
            src_ref=outgoing.at[direction, hop - 1, part],
            dst_ref=incoming.at[direction, hop - 1, part],
            send_sem=send_sems.at[direction, hop - 1, chunk],
            recv_sem=recv_sems.at[direction, hop - 1, chunk],
            device_id={"tp": ahead[direction]},
            device_id_type=pl.DeviceIdType.MESH,
        )

    def partial_sums(owners):
        for i, owner in enumerate(owners):
            picked[i * rows : (i + 1) * rows] = grads[
                pl.ds(pl.multiple_of(owner * rows, rows), rows)
            ]
        count = len(owners) * rows

        def column(j, carry):
            at = pl.ds(pl.multiple_of(j * tile, tile), tile)
            total[:count, at] = lax.dot_general(
                picked[:count],
                held[at, :],
                (((1,), (1,)), ((), ())),
                preferred_element_type=jnp.float32,
            )
            return carry

        lax.fori_loop(0, width // tile, column, 0)

    for copy in loads:
        copy.wait()
    sends = []
    for hop in range(last, 0, -1):
        owners = [ring_device(place + hop, n)]
        if hop < last:
            owners.append(ring_device(place - hop, n))
        partial_sums(owners)
        for position in (1, 0):
            for direction in range(2):
                order = chunks_of(direction, hop, last)
                if position < len(order):
                    chunk = order[position]
                    base = direction * rows if hop < last else 0
                    part = slice(chunk * half, (chunk + 1) * half)
                    value = total[base + chunk * half : base + (chunk + 1) * half]
                    if hop < last and chunk in chunks_of(direction, hop + 1, last):
                        sender(direction, hop + 1, chunk).wait_recv()
                        value = value + incoming[direction, hop, part].astype(jnp.float32)
                    outgoing[direction, hop - 1, part] = value.astype(jnp.bfloat16)
                    sends.append(sender(direction, hop, chunk))
                    sends[-1].start()
    partial_sums([lax.axis_index("tp")])
    for chunk in (1, 0):
        part = slice(chunk * half, (chunk + 1) * half)
        value = total[part]
        for direction in range(2):
            if chunk in chunks_of(direction, 1, last):
                sender(direction, 1, chunk).wait_recv()
                value = value + incoming[direction, 0, part].astype(jnp.float32)
        values = tokens[part].astype(jnp.float32)
        scale = lax.rsqrt(jnp.mean(values * values, axis=1, keepdims=True) + EPS)
        upper = value * gain[...]
        unit = values * scale
        out[part] = (
            scale * (upper - unit * jnp.mean(upper * unit, axis=1, keepdims=True))
        ).astype(jnp.bfloat16)
    for copy in sends:
        copy.wait_send()


def scatter_grads(grads, tokens, norm_gain, weights):
    n = lax.axis_size("tp")
    rows, width = tokens.shape
    cols = grads.shape[1]
    vmem = pl.BlockSpec(memory_space=pltpu.VMEM)
    hbm = pl.BlockSpec(memory_space=pl.ANY)
    return pl.pallas_call(
        functools.partial(scatter_kernel, n),
        out_shape=jax.ShapeDtypeStruct((rows, width), jnp.bfloat16),
        in_specs=[vmem, vmem, vmem, hbm, hbm, hbm],
        out_specs=vmem,
        scratch_shapes=[
            pltpu.VMEM((2, n // 2, rows, width), jnp.bfloat16),
            pltpu.VMEM((2, n // 2, rows, width), jnp.bfloat16),
            pltpu.VMEM((width, cols), jnp.bfloat16),
            pltpu.VMEM((2 * rows, cols), jnp.bfloat16),
            pltpu.VMEM((2 * rows, width), jnp.float32),
            pltpu.SemaphoreType.DMA((2, n // 2, 2)),
            pltpu.SemaphoreType.DMA((2, n // 2, 2)),
            pltpu.SemaphoreType.DMA((3,)),
        ],
        compiler_params=pltpu.CompilerParams(
            collective_id=1, has_side_effects=True, vmem_limit_bytes=VMEM_BYTES
        ),
        name="scatter_grads",
    )(grads, tokens, norm_gain.reshape(1, width), *weights)


def block_grads(query_blk, grad_blk, key_blk, value_blk, query_pos, key_pos):
    row_count = query_blk.shape[0]
    key_span = key_blk.shape[0]
    kv_heads = key_blk.shape[1] // HEAD_SIZE
    groups = query_blk.shape[1] // key_blk.shape[1]
    query_four = query_blk.reshape(row_count, kv_heads, groups, HEAD_SIZE)
    grad_four = grad_blk.reshape(row_count, kv_heads, groups, HEAD_SIZE)
    key_three = key_blk.reshape(key_span, kv_heads, HEAD_SIZE)
    value_three = value_blk.reshape(key_span, kv_heads, HEAD_SIZE)
    raw = jnp.einsum("qkgd,skd->kgqs", query_four, key_three, preferred_element_type=jnp.float32)
    bent = jnp.tanh(raw * SCALE / CAP)
    capped = CAP * bent
    valid = (
        (key_pos[None, :] <= query_pos[:, None])
        & (key_pos[None, :] > query_pos[:, None] - WINDOW)
        & (key_pos[None, :] >= 0)
    )
    expo = jnp.where(valid, jnp.exp(capped), 0.0)
    probs = expo / jnp.sum(expo, axis=-1, keepdims=True)
    d_probs = jnp.einsum(
        "qkgd,skd->kgqs", grad_four, value_three, preferred_element_type=jnp.float32
    )
    delta = jnp.sum(probs * d_probs, axis=-1, keepdims=True)
    d_raw = (probs * (d_probs - delta) * (1.0 - bent * bent) * SCALE).astype(jnp.bfloat16)
    probs_low = probs.astype(jnp.bfloat16)
    grad_query = jnp.einsum(
        "kgqs,skd->qkgd", d_raw, key_three, preferred_element_type=jnp.float32
    ).reshape(row_count, kv_heads * groups * HEAD_SIZE)
    grad_key = jnp.einsum(
        "kgqs,qkgd->skd", d_raw, query_four, preferred_element_type=jnp.float32
    ).reshape(key_span, kv_heads * HEAD_SIZE)
    grad_value = jnp.einsum(
        "kgqs,qkgd->skd", probs_low, grad_four, preferred_element_type=jnp.float32
    ).reshape(key_span, kv_heads * HEAD_SIZE)
    return (grad_query, grad_key, grad_value)


def on_device(tokens, norm_gain, query_weight, key_matrix, value_matrix, output_grad):
    local_rows = output_grad.shape[0]
    query_cols = query_weight.shape[1]
    key_cols = key_matrix.shape[1]
    reach = WINDOW - local_rows
    weights = (query_weight, key_matrix, value_matrix)
    joined = gather_project(tokens, norm_gain, weights)
    query_own = joined[:, :query_cols]
    pair_own = joined[:, query_cols:]
    near_pair = shifted(pair_own, "seq", 1)
    far_pair = shifted(pair_own[local_rows - reach :], "seq", 2)
    pairs = jnp.concatenate([far_pair, near_pair, pair_own], axis=0)
    anchor = lax.axis_index("seq") * local_rows
    query_pos = anchor + jnp.arange(local_rows, dtype=jnp.int32)
    key_pos = anchor - WINDOW + jnp.arange(WINDOW + local_rows, dtype=jnp.int32)
    grad_query, grad_key, grad_value = block_grads(
        query_own, output_grad, pairs[:, :key_cols], pairs[:, key_cols:], query_pos, key_pos
    )
    grad_pair = jnp.concatenate([grad_key, grad_value], axis=1)
    far_back = shifted(grad_pair[:reach], "seq", -2)
    back = shifted(grad_pair[reach:WINDOW], "seq", -1)
    own = grad_pair[WINDOW:] + back
    own = own.at[local_rows - reach :].add(far_back)
    grads = jnp.concatenate([grad_query.astype(jnp.bfloat16), own.astype(jnp.bfloat16)], axis=1)
    return scatter_grads(grads, tokens, norm_gain, weights)


def solution(mesh):
    return jax.shard_map(
        on_device,
        mesh=mesh,
        in_specs=(
            P(("seq", "tp"), None),
            P(),
            P(None, "tp"),
            P(None, "tp"),
            P(None, "tp"),
            P("seq", "tp"),
        ),
        out_specs=P(("seq", "tp"), None),
        check_vma=False,
    )
```

time: 377 us -> 196 us (0.52)
  waiting for transfers between devices: 244 us -> 12.1 us
  Pallas kernels: 0 us -> 114 us
  matrix products: 85.7 us -> 43.9 us
  between operations: 13.8 us -> 0.27 us
  starting transfers between devices: 14.9 us -> 8.31 us
  other arithmetic: 10.8 us -> 6.03 us
  local copies, waits for them, and re-layouts: 6.91 us -> 11.5 us
    reduce_scatter x1 -> x0, waiting for transfers between devices: 163 us -> none  [on_device(): lax.psum_scatter(total_term + row_product(value_low, value_matrix), 'tp',...]
    pallas_call x0 -> x2, Pallas kernels: none -> 114 us  [the longest x1 59.4 us: scatter_grads(): pl.pallas_call(functools.partial(scatter_kernel, n), out_shape=jax.ShapeD...]
    all_gather x1 -> x0, waiting for transfers between devices: 80.5 us -> none  [on_device(): lax.all_gather(tokens, 'tp', axis=0, tiled=True)]
    dot_general x6 -> x0, matrix products: 28.7 us -> none  [the longest x3 19.2 us: row_product(): lax.dot_general(grad_rows, weight, (((1,), (1,)), ((), ())), preferred_el...]
    ppermute x8 -> x4, waiting for transfers between devices: 0.02 us -> 12.1 us  [shifted(): return lax.ppermute(block, axis, route)]
    dot_general x1, matrix products: 22.3 us -> 15.6 us  [block_grads(): jnp.einsum('kgqs,qkgd->skd', d_raw, query_four, preferred_element_type=jn...]
    ppermute x8 -> x4, starting transfers between devices: 14.9 us -> 8.31 us  [shifted(): return lax.ppermute(block, axis, route)]
    reduce_sum x3 -> x0, other arithmetic: 5.31 us -> none  [the longest x1 3.48 us: normalize_project(): jnp.mean(float_values * float_values, axis=1, keepdims=True) + EPS]
  transfers between devices with their start and end apart: 10 -> 4, of which waited for: 2 -> 1; matrix products, arithmetic and copies ran while one was open for 6% -> 11% of each run, Pallas kernels for 0% -> 0%
where the time goes in v1:
time: 196 us
  Pallas kernels  114 us (58%)
  matrix products  43.9 us (22%)
  waiting for transfers between devices  12.1 us (6%)
  local copies, waits for them, and re-layouts  11.5 us (6%)
  starting transfers between devices  8.31 us (4%)
  other arithmetic  6.03 us (3%)
    pallas_call x1, Pallas kernels, scatter_grads(): pl.pallas_call(functools.partial(scatter_kernel, n), out_shape=jax.ShapeD...  59.4 us
    pallas_call x1, Pallas kernels, gather_project(): pl.pallas_call(functools.partial(gather_kernel, n), out_shape=jax.ShapeDt...  54.2 us
    dot_general x1, matrix products, block_grads(): jnp.einsum('kgqs,skd->qkgd', d_raw, key_three, preferred_element_type=jnp...  16.8 us
    dot_general x1, matrix products, block_grads(): jnp.einsum('kgqs,qkgd->skd', d_raw, query_four, preferred_element_type=jn...  15.6 us
    ppermute x4, waiting for transfers between devices, shifted(): return lax.ppermute(block, axis, route)  12.1 us
    ppermute x4, starting transfers between devices, shifted(): return lax.ppermute(block, axis, route)  8.31 us
    unnamed x13, local copies, waits for them, and re-layouts  5.57 us
    dot_general x1, matrix products, block_grads(): jnp.einsum('qkgd,skd->kgqs', grad_four, value_three, preferred_element_ty...  4.99 us
  transfers between devices with their start and end apart: 4, of which 1 were waited for; matrix products, arithmetic and copies ran while one was open for 11% of the time, Pallas kernels for 0%

profile of v1, /device:TPU:0, one launch (start us, length us, event | category | flops | bytes accessed | tf_op | source)
XLA Modules:
  0.0 195.8 jit_solution(7854525322770041325)
XLA Ops:
  0.0 1.4 reshape.68.gain
  1.4 54.2 %gather_project.1 = bf16[512,1024]{1,0:T(8,128)(2,1)} custom-call(bf16[64,4608]{1,0:T(8,128)(2,1)} %tokens.3, f32[1,4608]{1,0:T(1,128)} %reshape.68.gain, bf16[4608,512]{1,0:T(8,128)(2,1)} %wq.3, bf16[4608,256]{1,0:T(8,128)(2,1)} %wk.3, bf16[4608,256]{1,0:T(8,128)(2,1)} %wv.3), custom_call_target="tpu_custom_call" | custom-call | tf_op jit(solution)/shard_map/gather_project/pallas_call | solution.py:145
  55.6 0.9 slice.44
  56.5 3.4 %collective-permute-start = (bf16[128,512]{1,0:T(8,128)(2,1)S(1)}, bf16[128,512]{1,0:T(8,128)(2,1)S(1)}, u32[]{:S(2)}, u32[]{:S(2)}) collective-permute-start(bf16[128,512]{1,0:T(8,128)(2,1)S(1)} %slice.44), channel_id=1, source_target_pairs={{0,16},{8,24},{1,17},{9,25},{2,18},{10,26},{3,19},{11,27},{4,20},{... | collective-permute-start | bytes 393224 | tf_op jit(solution)/shard_map/ppermute | solution.py:23
  60.0 1.3 fusion.32
  61.2 2.1 %collective-permute-start.1 = (bf16[512,512]{1,0:T(8,128)(2,1)S(1)}, bf16[512,512]{1,0:T(8,128)(2,1)}, u32[]{:S(2)}, u32[]{:S(2)}) collective-permute-start(bf16[512,512]{1,0:T(8,128)(2,1)S(1)} %get-tuple-element.19), channel_id=1, source_target_pairs={{0,8},{8,16},{16,24},{1,9},{9,17},{17,25},{2,10},{10,18},{18,26},{... | collective-permute-start | bytes 1572872 | tf_op jit(solution)/shard_map/ppermute | solution.py:23
  63.3 0.9 and_and_fusion
  64.8 1.3 pad_maximum_fusion
  66.3 0.6 copy.22
  67.1 5.0 %fusion.15 = f32[2,1152,512,2]{2,1,3,0:T(8,128)} fusion(bf16[512,2,2,128]{0,3,2,1:T(8,128)(2,1)S(1)} %bitcast.87, bf16[1152,2,128,1]{2,1,0,3:T(2,128)(2,1)S(1)} %bitcast.85), kind=kOutput, calls=%fused_computation.27 | convolution fusion | flops 603979776 | bytes 10551296 | tf_op jit(solution)/shard_map/qkgd,skd->kgqs/dot_general | solution.py:310
  72.1 3.2 %fusion.5 = (f32[2,2,512]{2,1,0:T(2,128)S(1)}, f32[2,1152,512,2]{2,1,3,0:T(8,128)S(1)}) fusion(pred[512,1152]{0,1:T(8,128)(4,1)S(1)} %and_and_fusion, bf16[1152,2,128,1]{0,2,3,1:T(8,128)(2,1)S(1)} %copy.22, bf16[512,2,2,128]{0,3,2,1:T(8,128)(2,1)S(1)} %bitcast.91), kind=kOutput, calls=%fused_computation.10 | convolution fusion | flops 613414912 | bytes 11149312 | tf_op jit(solution)/shard_map/qkgd,skd->kgqs/dot_general | solution.py:300
  75.3 3.6 %copy-done.5 = f32[2,1152,512,2]{2,1,3,0:T(8,128)} copy-done((f32[2,1152,512,2]{2,1,3,0:T(8,128)}, f32[2,1152,512,2]{2,1,3,0:T(8,128)S(1)}, u32[]{:S(2)}) %copy-start.5) | copy-done | bytes 9437208
  78.9 3.4 %fusion.6 = f32[2,1152,128,1]{1,2,3,0:T(8,128)S(1)} fusion(bf16[512,2,2,128]{0,3,2,1:T(8,128)(2,1)S(1)} %bitcast.88, f32[2,1152,512,2]{2,1,3,0:T(8,128)S(1)} %get-tuple-element.22, f32[2,2,512]{2,1,0:T(2,128)S(1)} %get-tuple-element.21, pred[512,1152]{0,1:T(8,128)(4,1)S(1)} %and_and_fusion), kind=kOutput, calls=%fused_computation.11 | convolution fusion | flops 615776256 | bytes 11739136 | tf_op jit(solution)/shard_map/kgqs,qkgd->skd/dot_general | solution.py:322
  82.3 15.6 %fusion.9 = f32[2,128,1152,1]{2,1,3,0:T(8,128)S(1)} fusion(bf16[512,2,2,128]{0,3,2,1:T(8,128)(2,1)S(1)} %bitcast.92, f32[2,1152,512,2]{2,1,3,0:T(8,128)} %fusion.15, f32[2,1152,512,2]{2,1,3,0:T(8,128)} %copy-done.5, f32[2,2,512]{2,1,0:T(2,128)S(1)} %get-tuple-element.21, pred[512,1152]{0,1:T(8,128)(4,1)} %copy-done), kind=kOutput, calls=%fused_computation.19 | convolution fusion | flops 641731712 | bytes 21176320 | tf_op jit(solution)/shard_map/kgqs,qkgd->skd/dot_general | solution.py:319
  97.9 0.4 copy.36
  98.7 1.1 fusion.12
  99.8 1.5 collective-permute-start.2
  101.3 16.8 %fusion.11 = bf16[2,128,2,512]{3,1,2,0:T(8,128)(2,1)S(1)} fusion(bf16[1152,2,128,1]{0,2,3,1:T(8,128)(2,1)} %copy-done.1, f32[2,1152,512,2]{2,1,3,0:T(8,128)} %fusion.15, f32[2,1152,512,2]{2,1,3,0:T(8,128)} %copy-done.5, f32[2,2,512]{2,1,0:T(2,128)S(1)} %get-tuple-element.21, pred[512,1152]{0,1:T(8,128)(4,1)} %copy-done), kind=kOutput, calls=%fused_computation.21 | convolution fusion | flops 641993856 | bytes 20586496 | tf_op jit(solution)/shard_map/kgqs,skd->qkgd/dot_general | solution.py:316
  118.4 1.3 collective-permute-start.3
  119.7 1.4 fusion.14
  121.1 12.1 %collective-permute-done.3 = f32[128,512]{1,0:T(8,128)S(1)} collective-permute-done((f32[128,512]{1,0:T(8,128)S(1)}, f32[128,512]{1,0:T(8,128)S(1)}, u32[]{:S(2)}, u32[]{:S(2)}) %collective-permute-start.3) | collective-permute-done | bytes 262176 | tf_op jit(solution)/shard_map/ppermute | solution.py:23
  133.3 1.1 pad_maximum_fusion.1.grads
  134.4 59.4 %scatter_grads.1 = bf16[64,4608]{1,0:T(8,128)(2,1)} custom-call(bf16[512,1024]{1,0:T(8,128)(2,1)} %pad_maximum_fusion.1.grads, bf16[64,4608]{1,0:T(8,128)(2,1)} %tokens.3, f32[1,4608]{1,0:T(1,128)} %reshape.68.gain, bf16[4608,512]{1,0:T(8,128)(2,1)} %wq.3, bf16[4608,256]{1,0:T(8,128)(2,1)} %wk.3, bf16[4608,256]{1,0:T(8,128)(2,1)} %wv.3), custom_call_target="tpu_custom_call" | custom-call | tf_op jit(solution)/shard_map/scatter_grads/pallas_call | solution.py:269
  193.9 1.9 copy.43
  (27 shorter events, 1.6 us)
Async XLA Ops:
  0.0 64.3 %copy-start.2 = (bf16[512,512]{1,0:T(8,128)(2,1)S(1)}, bf16[512,512]{1,0:T(8,128)(2,1)}, u32[]{:S(2)}) copy-start(bf16[512,512]{1,0:T(8,128)(2,1)} %param.13) | copy-start | bytes 1572868
  56.5 8.2 %collective-permute-start = (bf16[128,512]{1,0:T(8,128)(2,1)S(1)}, bf16[128,512]{1,0:T(8,128)(2,1)S(1)}, u32[]{:S(2)}, u32[]{:S(2)}) collective-permute-start(bf16[128,512]{1,0:T(8,128)(2,1)S(1)} %slice.44), channel_id=1, source_target_pairs={{0,16},{8,24},{1,17},{9,25},{2,18},{10,26},{3,19},{11,27},{4,20},{... | collective-permute-start | bytes 393224 | tf_op jit(solution)/shard_map/ppermute | solution.py:23
  61.2 3.5 %collective-permute-start.1 = (bf16[512,512]{1,0:T(8,128)(2,1)S(1)}, bf16[512,512]{1,0:T(8,128)(2,1)}, u32[]{:S(2)}, u32[]{:S(2)}) collective-permute-start(bf16[512,512]{1,0:T(8,128)(2,1)S(1)} %get-tuple-element.19), channel_id=1, source_target_pairs={{0,8},{8,16},{16,24},{1,9},{9,17},{17,25},{2,10},{10,18},{18,26},{... | collective-permute-start | bytes 1572872 | tf_op jit(solution)/shard_map/ppermute | solution.py:23
  64.3 11.0 %copy-start = (pred[512,1152]{0,1:T(8,128)(4,1)}, pred[512,1152]{0,1:T(8,128)(4,1)S(1)}, u32[]{:S(2)}) copy-start(pred[512,1152]{0,1:T(8,128)(4,1)S(1)} %and_and_fusion) | copy-start | bytes 1769476
  64.7 10.5 %copy-start.3 = (bf16[512,512]{0,1:T(8,128)(2,1)}, bf16[512,512]{0,1:T(8,128)(2,1)S(1)}, u32[]{:S(2)}) copy-start(bf16[512,512]{0,1:T(8,128)(2,1)S(1)} %copy.37) | copy-start | bytes 1572868
  66.9 8.3 %copy-start.1 = (bf16[1152,2,128,1]{0,2,3,1:T(8,128)(2,1)}, bf16[1152,2,128,1]{0,2,3,1:T(8,128)(2,1)S(1)}, u32[]{:S(2)}) copy-start(bf16[1152,2,128,1]{0,2,3,1:T(8,128)(2,1)S(1)} %copy.22) | copy-start | bytes 1769476
  75.3 3.6 %copy-start.5 = (f32[2,1152,512,2]{2,1,3,0:T(8,128)}, f32[2,1152,512,2]{2,1,3,0:T(8,128)S(1)}, u32[]{:S(2)}) copy-start(f32[2,1152,512,2]{2,1,3,0:T(8,128)S(1)} %get-tuple-element.22) | copy-start | bytes 28311556
  78.9 3.4 %copy-start.4 = (bf16[512,512]{0,1:T(8,128)(2,1)S(1)}, bf16[512,512]{0,1:T(8,128)(2,1)}, u32[]{:S(2)}) copy-start(bf16[512,512]{0,1:T(8,128)(2,1)} %copy-done.3) | copy-start | bytes 1572868
  99.8 19.8 %collective-permute-start.2 = (f32[512,512]{1,0:T(8,128)}, f32[512,512]{1,0:T(8,128)}, u32[]{:S(2)}, u32[]{:S(2)}) collective-permute-start(f32[512,512]{1,0:T(8,128)} %fusion.12), channel_id=1, source_target_pairs={{8,0},{16,8},{24,16},{9,1},{17,9},{25,17},{10,2},{18,10},{26,18},{... | collective-permute-start | bytes 3145736 | tf_op jit(solution)/shard_map/ppermute | solution.py:23
  118.4 14.8 %collective-permute-start.3 = (f32[128,512]{1,0:T(8,128)S(1)}, f32[128,512]{1,0:T(8,128)S(1)}, u32[]{:S(2)}, u32[]{:S(2)}) collective-permute-start(f32[128,512]{1,0:T(8,128)S(1)} %pad_maximum_fusion.2), channel_id=1, source_target_pairs={{16,0},{24,8},{17,1},{25,9},{18,2},{26,10},{19,3},{27,11},{20,4},{... | collective-permute-start | bytes 786440 | tf_op jit(solution)/shard_map/ppermute | solution.py:23

commit v2 on v1

v2 whole, which is shorter than its diff:
```python
import functools
import types

import jax
import jax.numpy as jnp
from jax import lax
from jax.experimental import pallas as pl
from jax.experimental.pallas import tpu as pltpu
from jax.sharding import PartitionSpec as P

HEAD_SIZE = 128
WINDOW = 640


SCALE = 1.0 / 12.0
CAP = 50.0
EPS = 1e-06
VMEM_BYTES = 60 * 1024 * 1024
QUERY_ROWS = 128
TILE = 256


def ring_place(index, n):
    odd = index % 2
    return (1 - odd) * (index // 2) + odd * (n - 1 - index // 2)


def ring_device(place, n):
    place = (place + n) % n
    late = place // (n // 2)
    return (1 - late) * 2 * place + late * (2 * (n - 1 - place) + 1)


def chunks_of(direction, hop, last):
    return (direction, 1 - direction) if hop < last else (direction,)


def greet(neighbours):
    barrier = pltpu.get_barrier_semaphore()
    for neighbour in neighbours:
        pl.semaphore_signal(
            barrier, inc=1, device_id=neighbour, device_id_type=pl.DeviceIdType.MESH
        )
    pl.semaphore_wait(barrier, len(neighbours))


def remote(source, target, send_sem, recv_sem, device):
    return pltpu.make_async_remote_copy(
        src_ref=source,
        dst_ref=target,
        send_sem=send_sem,
        recv_sem=recv_sem,
        device_id=device,
        device_id_type=pl.DeviceIdType.MESH,
    )


def load_weights(weights, held, sems):
    copies = []
    start = 0
    for i, weight in enumerate(weights):
        cols = weight.shape[1]
        copies.append(
            pltpu.make_async_copy(weight, held.at[:, start : start + cols], sems.at[i])
        )
        start += cols
    for copy in copies:
        copy.start()
    return copies


def rows_at(index, count):
    return pl.ds(pl.multiple_of(index * count, count), count)


def gather_phase(n, ring, onward, tokens, gain, loads, s):
    rows, _ = tokens.shape
    local = n * rows
    half = rows // 2
    last = n // 2
    query_cols = s.query.shape[1]
    pair_cols = s.pairs.shape[1]
    me = lax.axis_index("tp")
    place = ring_place(me, n)
    sends = []
    halos = []

    def sender(direction, hop, chunk):
        step = -(hop - 1) if direction == 0 else hop - 1
        owner = ring_device(place + step, n)
        part = pl.ds(chunk * half, half)
        return remote(
            tokens.at[part] if hop == 1 else s.gathered.at[owner, part],
            s.gathered.at[owner, part],
            s.gather_send.at[direction, hop - 1, chunk],
            s.gather_recv.at[direction, hop - 1, chunk],
            ring[direction],
        )

    def project(sources):
        for i, (block, _) in enumerate(sources):
            values = block[...].astype(jnp.float32)
            scale = lax.rsqrt(jnp.mean(values * values, axis=1, keepdims=True) + EPS)
            s.normed[i * rows : (i + 1) * rows] = (values * scale * gain[...]).astype(jnp.bfloat16)
        count = len(sources) * rows

        def column(target, base, first):
            def write(j, carry):
                product = jnp.dot(
                    s.normed[:count],
                    s.held[:, pl.ds(pl.multiple_of(first + j * TILE, TILE), TILE)],
                    preferred_element_type=jnp.float32,
                ).astype(jnp.bfloat16)
                for i, (_, owner) in enumerate(sources):
                    at = pl.ds(pl.multiple_of(base + owner * rows, rows), rows)
                    target[at, rows_at(j, TILE)] = product[i * rows : (i + 1) * rows]
                return carry

            return write

        lax.fori_loop(0, pair_cols // TILE, column(s.pairs, 2 * local, query_cols), 0)
        for _, owner in sources:
            for back in range(2):
                source = pl.ds(pl.multiple_of(2 * local + owner * rows, rows), rows)
                target = pl.ds(pl.multiple_of((1 - back) * local + owner * rows, rows), rows)
                halos.append(
                    remote(
                        s.pairs.at[source],
                        s.pairs.at[target],
                        s.halo_send.at[back, len(halos) // 2],
                        s.halo_recv.at[back, len(halos) // 2],
                        onward[back],
                    )
                )
                halos[-1].start()
        lax.fori_loop(0, query_cols // TILE, column(s.query, 0, 0), 0)

    for position in range(2):
        for direction in range(2):
            order = chunks_of(direction, 1, last)
            if position < len(order):
                sends.append(sender(direction, 1, order[position]))
                sends[-1].start()
    for copy in loads:
        copy.wait()
    project([(tokens, me)])
    for hop in range(1, last + 1):
        for position in range(2):
            for direction in range(2):
                order = chunks_of(direction, hop, last)
                if position < len(order):
                    chunk = order[position]
                    sender(direction, hop, chunk).wait_recv()
                    if hop < last and chunk in chunks_of(direction, hop + 1, last):
                        sends.append(sender(direction, hop + 1, chunk))
                        sends[-1].start()
        owners = [ring_device(place - hop, n)]
        if hop < last:
            owners.append(ring_device(place + hop, n))
        project([(s.gathered.at[owner], owner) for owner in owners])
    for copy in halos:
        copy.wait_recv()
    return sends + halos


def dot(lhs, rhs, left, right):
    return lax.dot_general(
        lhs, rhs, (((left,), (right,)), ((), ())), preferred_element_type=jnp.float32
    )


def attention_phase(backward, output_grad, s):
    local, query_cols = s.query.shape
    key_cols = s.pairs.shape[1] // 2
    kv_heads = key_cols // HEAD_SIZE
    groups = query_cols // key_cols
    reach = WINDOW - local
    span = WINDOW + QUERY_ROWS
    start = 2 * local - WINDOW
    anchor = lax.axis_index("seq") * local
    shape = (span, groups * QUERY_ROWS)
    key_at = lax.broadcasted_iota(jnp.int32, shape, 0)
    gap = key_at - lax.broadcasted_iota(jnp.int32, shape, 1) % QUERY_ROWS
    s.band[...] = jnp.where((gap > 0) & (gap <= WINDOW), key_at, -1)
    s.sums[...] = jnp.zeros_like(s.sums)
    sends = []

    def halo(head, back):
        part = pl.ds(reach, local) if back == 0 else pl.ds(0, reach)
        return remote(
            s.leaving.at[head, part],
            s.arriving.at[head, part],
            s.back_send.at[head, back],
            s.back_recv.at[head, back],
            backward[back],
        )

    for head in range(kv_heads):
        key_lanes = slice(head * HEAD_SIZE, (head + 1) * HEAD_SIZE)
        value_lanes = slice(key_cols + head * HEAD_SIZE, key_cols + (head + 1) * HEAD_SIZE)
        heads = [
            slice((head * groups + g) * HEAD_SIZE, (head * groups + g + 1) * HEAD_SIZE)
            for g in range(groups)
        ]

        def block(i, carry):
            own = rows_at(i, QUERY_ROWS)
            seen = pl.ds(pl.multiple_of(start + i * QUERY_ROWS, QUERY_ROWS), span)
            query = jnp.concatenate([s.query[own, lanes] for lanes in heads], axis=0)
            grad = jnp.concatenate([output_grad[own, lanes] for lanes in heads], axis=0)
            key = s.pairs[seen, key_lanes]
            value = s.pairs[seen, value_lanes]
            bent = jnp.tanh(dot(key, query, 1, 1) * (SCALE / CAP))
            first = jnp.maximum(WINDOW - anchor - i * QUERY_ROWS, 0)
            expo = jnp.where(s.band[...] >= first, jnp.exp(CAP * bent), 0.0)
            probs = expo * (1.0 / jnp.sum(expo, axis=0, keepdims=True))
            d_probs = dot(value, grad, 1, 1)
            delta = jnp.sum(probs * d_probs, axis=0, keepdims=True)
            d_raw = (probs * (d_probs - delta) * (1.0 - bent * bent) * SCALE).astype(jnp.bfloat16)
            at = pl.ds(pl.multiple_of(i * QUERY_ROWS, QUERY_ROWS), span)
            s.sums[head, at, :HEAD_SIZE] += dot(d_raw, query, 1, 0)
            s.sums[head, at, HEAD_SIZE:] += dot(probs.astype(jnp.bfloat16), grad, 1, 0)
            grad_query = dot(d_raw, key, 0, 0).astype(jnp.bfloat16)
            for g, lanes in enumerate(heads):
                s.grads[own, lanes] = grad_query[g * QUERY_ROWS : (g + 1) * QUERY_ROWS]
            return carry

        lax.fori_loop(0, local // QUERY_ROWS, block, 0)
        s.leaving[head] = s.sums[head, :WINDOW].astype(jnp.bfloat16)
        for back in range(2):
            sends.append(halo(head, back))
            sends[-1].start()
    for head in range(kv_heads):
        for back in range(2):
            halo(head, back).wait_recv()
        s.sums[head, WINDOW:] += s.arriving[head, reach:].astype(jnp.float32)
        s.sums[head, WINDOW + local - reach :] += s.arriving[head, :reach].astype(jnp.float32)
        for side in range(2):
            lanes = slice(side * HEAD_SIZE, (side + 1) * HEAD_SIZE)
            column = query_cols + side * key_cols + head * HEAD_SIZE
            s.grads[:, column : column + HEAD_SIZE] = s.sums[head, WINDOW:, lanes].astype(
                jnp.bfloat16
            )
    return sends


def scatter_phase(n, ring, tokens, gain, out, s):
    rows, width = tokens.shape
    half = rows // 2
    last = n // 2
    me = lax.axis_index("tp")
    place = ring_place(me, n)

    def sender(direction, hop, chunk):
        part = pl.ds(chunk * half, half)
        return remote(
            s.outgoing.at[direction, hop - 1, part],
            s.incoming.at[direction, hop - 1, part],
            s.scatter_send.at[direction, hop - 1, chunk],
            s.scatter_recv.at[direction, hop - 1, chunk],
            ring[direction],
        )

    def partial_sums(owners):
        for i, owner in enumerate(owners):
            s.picked[i * rows : (i + 1) * rows] = s.grads[rows_at(owner, rows)]
        count = len(owners) * rows

        def column(j, carry):
            at = rows_at(j, TILE)
            s.total[:count, at] = dot(s.picked[:count], s.held[at, :], 1, 1)
            return carry

        lax.fori_loop(0, width // TILE, column, 0)

    sends = []
    for hop in range(last, 0, -1):
        owners = [ring_device(place + hop, n)]
        if hop < last:
            owners.append(ring_device(place - hop, n))
        partial_sums(owners)
        for position in (1, 0):
            for direction in range(2):
                order = chunks_of(direction, hop, last)
                if position < len(order):
                    chunk = order[position]
                    base = direction * rows if hop < last else 0
                    part = slice(chunk * half, (chunk + 1) * half)
                    value = s.total[base + chunk * half : base + (chunk + 1) * half]
                    if hop < last and chunk in chunks_of(direction, hop + 1, last):
                        sender(direction, hop + 1, chunk).wait_recv()
                        value = value + s.incoming[direction, hop, part].astype(jnp.float32)
                    s.outgoing[direction, hop - 1, part] = value.astype(jnp.bfloat16)
                    sends.append(sender(direction, hop, chunk))
                    sends[-1].start()
    partial_sums([me])
    for chunk in (1, 0):
        part = slice(chunk * half, (chunk + 1) * half)
        value = s.total[part]
        for direction in range(2):
            if chunk in chunks_of(direction, 1, last):
                sender(direction, 1, chunk).wait_recv()
                value = value + s.incoming[direction, 0, part].astype(jnp.float32)
        values = tokens[part].astype(jnp.float32)
        scale = lax.rsqrt(jnp.mean(values * values, axis=1, keepdims=True) + EPS)
        upper = value * gain[...]
        unit = values * scale
        out[part] = (
            scale * (upper - unit * jnp.mean(upper * unit, axis=1, keepdims=True))
        ).astype(jnp.bfloat16)
    return sends


def kernel(names, n, seqs, tokens, gain, output_grad, wq, wk, wv, out, *scratch):
    s = types.SimpleNamespace(**dict(zip(names, scratch)))
    loads = load_weights((wq, wk, wv), s.held, s.load_sems)
    place = ring_place(lax.axis_index("tp"), n)
    block = lax.axis_index("seq")
    ring = [{"tp": ring_device(place + step, n)} for step in (1, -1)]
    onward = [{"seq": (block + step) % seqs} for step in (1, 2)]
    backward = [{"seq": (block + seqs - step) % seqs} for step in (1, 2)]
    greet(ring + onward + backward)
    sends = gather_phase(n, ring, onward, tokens, gain, loads, s)
    sends += attention_phase(backward, output_grad, s)
    sends += scatter_phase(n, ring, tokens, gain, out, s)
    for copy in sends:
        copy.wait_send()


def on_device(tokens, norm_gain, query_weight, key_matrix, value_matrix, output_grad):
    n = lax.axis_size("tp")
    rows, width = tokens.shape
    local, query_cols = output_grad.shape
    key_cols = key_matrix.shape[1]
    cols = query_cols + 2 * key_cols
    kv_heads = key_cols // HEAD_SIZE
    groups = query_cols // key_cols
    low, full = jnp.bfloat16, jnp.float32
    hops = pltpu.SemaphoreType.DMA((2, n // 2, 2))
    blocks = pltpu.SemaphoreType.DMA((2, n))
    heads = pltpu.SemaphoreType.DMA((kv_heads, 2))
    scratch = dict(
        gathered=pltpu.VMEM((n, rows, width), low),
        held=pltpu.VMEM((width, cols), low),
        normed=pltpu.VMEM((2 * rows, width), low),
        query=pltpu.VMEM((local, query_cols), low),
        pairs=pltpu.VMEM((3 * local, 2 * key_cols), low),
        band=pltpu.VMEM((WINDOW + QUERY_ROWS, groups * QUERY_ROWS), jnp.int32),
        sums=pltpu.VMEM((kv_heads, WINDOW + local, 2 * HEAD_SIZE), full),
        leaving=pltpu.VMEM((kv_heads, WINDOW, 2 * HEAD_SIZE), low),
        arriving=pltpu.VMEM((kv_heads, WINDOW, 2 * HEAD_SIZE), low),
        grads=pltpu.VMEM((local, cols), low),
        outgoing=pltpu.VMEM((2, n // 2, rows, width), low),
        incoming=pltpu.VMEM((2, n // 2, rows, width), low),
        picked=pltpu.VMEM((2 * rows, cols), low),
        total=pltpu.VMEM((2 * rows, width), full),
        gather_send=hops,
        gather_recv=hops,
        halo_send=blocks,
        halo_recv=blocks,
        back_send=heads,
        back_recv=heads,
        scatter_send=hops,
        scatter_recv=hops,
        load_sems=pltpu.SemaphoreType.DMA((3,)),
    )
    vmem = pl.BlockSpec(memory_space=pltpu.VMEM)
    hbm = pl.BlockSpec(memory_space=pl.ANY)
    return pl.pallas_call(
        functools.partial(kernel, tuple(scratch), n, lax.axis_size("seq")),
        out_shape=jax.ShapeDtypeStruct((rows, width), low),
        in_specs=[vmem, vmem, vmem, hbm, hbm, hbm],
        out_specs=vmem,
        scratch_shapes=list(scratch.values()),
        compiler_params=pltpu.CompilerParams(
            collective_id=0, has_side_effects=True, vmem_limit_bytes=VMEM_BYTES
        ),
        name="attention_backward",
    )(tokens, norm_gain.reshape(1, width), output_grad, query_weight, key_matrix, value_matrix)


def solution(mesh):
    return jax.shard_map(
        on_device,
        mesh=mesh,
        in_specs=(
            P(("seq", "tp"), None),
            P(),
            P(None, "tp"),
            P(None, "tp"),
            P(None, "tp"),
            P("seq", "tp"),
        ),
        out_specs=P(("seq", "tp"), None),
        check_vma=False,
    )
```

time: 196 us -> 129 us (0.66)
  matrix products: 43.9 us -> 0 us
  waiting for transfers between devices: 12.1 us -> 0 us
  Pallas kernels: 114 us -> 125 us
  starting transfers between devices: 8.31 us -> 0 us
  local copies, waits for them, and re-layouts: 11.5 us -> 3.26 us
  other arithmetic: 6.03 us -> 0 us
    dot_general x5 -> x0, matrix products: 43.9 us -> none  [the longest x1 16.8 us: block_grads(): jnp.einsum('kgqs,skd->qkgd', d_raw, key_three, preferred_element_type=jnp...]
    ppermute x4 -> x0, waiting for transfers between devices: 12.1 us -> none  [shifted(): return lax.ppermute(block, axis, route)]
    pallas_call x2 -> x1, Pallas kernels: 114 us -> 125 us  [on_device(): pl.pallas_call(functools.partial(kernel, tuple(scratch), n, lax.axis_size...]
    ppermute x4 -> x0, starting transfers between devices: 8.31 us -> none  [shifted(): return lax.ppermute(block, axis, route)]
    unnamed x13 -> x1, local copies, waits for them, and re-layouts: 5.57 us -> 1.92 us
    concatenate x4 -> x0, other arithmetic: 3.58 us -> none  [the longest x1 1.3 us: on_device(): pairs = jnp.concatenate([far_pair, near_pair, pair_own], axis=0)]
    slice x3 -> x0, local copies, waits for them, and re-layouts: 2.26 us -> none  [the longest x1 1.27 us: on_device(): pair_own = joined[:, query_cols:]]
    reshape x8 -> x1, local copies, waits for them, and re-layouts: 3.46 us -> 1.35 us  [on_device(): norm_gain.reshape(1, width)]
  transfers between devices with their start and end apart: 4 -> 0, of which waited for: 1 -> 0; matrix products, arithmetic and copies ran while one was open for 11% -> 0% of each run, Pallas kernels for 0% -> 0%
where the time goes in v2:
time: 129 us
  Pallas kernels  125 us (97%)
  local copies, waits for them, and re-layouts  3.26 us (3%)
    pallas_call x1, Pallas kernels, on_device(): pl.pallas_call(functools.partial(kernel, tuple(scratch), n, lax.axis_size...  125 us

profile of v2, /device:TPU:0, one launch (start us, length us, event | category | flops | bytes accessed | tf_op | source)
XLA Modules:
  0.0 128.7 jit_solution(1174047352960094279)
XLA Ops:
  0.0 1.3 %reshape.3.gain = f32[1,4608]{1,0:T(1,128)} reshape(f32[4608]{0:T(1024)} %param.7) | data formatting | bytes 36864 | tf_op jit(solution)/shard_map/reshape | solution.py:379
  1.3 125.5 %attention_backward.1 = bf16[64,4608]{1,0:T(8,128)(2,1)} custom-call(bf16[64,4608]{1,0:T(8,128)(2,1)} %tokens.1, f32[1,4608]{1,0:T(1,128)} %reshape.3.gain, bf16[512,512]{1,0:T(8,128)(2,1)} %output_grad.1, bf16[4608,512]{1,0:T(8,128)(2,1)} %wq.1, bf16[4608,256]{1,0:T(8,128)(2,1)} %wk.1, bf16[4608,256]{1,0:T(8,128)(2,1)} %wv.1), custom_call_target="tpu_custom_call" | custom-call | tf_op jit(solution)/shard_map/attention_backward/pallas_call | solution.py:369
  126.8 1.9 %copy.8 = bf16[64,4608]{1,0:T(8,128)(2,1)} copy(bf16[64,4608]{1,0:T(8,128)(2,1)} %attention_backward.1) | data formatting | bytes 1179648

commit v3 on v2

--- a/solution.py
+++ b/solution.py
@@ -169,7 +169,7 @@
     )
 
 
-def attention_phase(backward, output_grad, s):
+def attention_phase(backward, output_grad, s, meanwhile):
     local, query_cols = s.query.shape
     key_cols = s.pairs.shape[1] // 2
     kv_heads = key_cols // HEAD_SIZE
@@ -185,13 +185,17 @@
     s.sums[...] = jnp.zeros_like(s.sums)
     sends = []
 
-    def halo(head, back):
-        part = pl.ds(reach, local) if back == 0 else pl.ds(0, reach)
+    early = local // QUERY_ROWS - 1
+    pieces = ((0, reach, 1), (reach, early * QUERY_ROWS, 0), (early * QUERY_ROWS, WINDOW, 0))
+
+    def halo(head, piece):
+        first, end, back = pieces[piece]
+        part = pl.ds(first, end - first)
         return remote(
             s.leaving.at[head, part],
             s.arriving.at[head, part],
-            s.back_send.at[head, back],
-            s.back_recv.at[head, back],
+            s.back_send.at[head, piece],
+            s.back_recv.at[head, piece],
             backward[back],
         )
 
@@ -225,14 +229,17 @@
                 s.grads[own, lanes] = grad_query[g * QUERY_ROWS : (g + 1) * QUERY_ROWS]
             return carry
 
-        lax.fori_loop(0, local // QUERY_ROWS, block, 0)
-        s.leaving[head] = s.sums[head, :WINDOW].astype(jnp.bfloat16)
-        for back in range(2):
-            sends.append(halo(head, back))
-            sends[-1].start()
+        for blocks, ready in (((0, early), (0, 1)), ((early, early + 1), (2,))):
+            lax.fori_loop(*blocks, block, 0)
+            for piece in ready:
+                first, end, _ = pieces[piece]
+                s.leaving[head, first:end] = s.sums[head, first:end].astype(jnp.bfloat16)
+                sends.append(halo(head, piece))
+                sends[-1].start()
+    meanwhile()
     for head in range(kv_heads):
-        for back in range(2):
-            halo(head, back).wait_recv()
+        for piece in range(len(pieces)):
+            halo(head, piece).wait_recv()
         s.sums[head, WINDOW:] += s.arriving[head, reach:].astype(jnp.float32)
         s.sums[head, WINDOW + local - reach :] += s.arriving[head, :reach].astype(jnp.float32)
         for side in range(2):
@@ -244,10 +251,27 @@
     return sends
 
 
+def farthest_query_sums(n, rows, s):
+    query_cols = s.query.shape[1]
+    place = ring_place(lax.axis_index("tp"), n)
+    s.picked[:rows, :query_cols] = s.grads[
+        rows_at(ring_device(place + n // 2, n), rows), :query_cols
+    ]
+
+    def column(j, carry):
+        at = rows_at(j, TILE)
+        s.total[:rows, at] = dot(s.picked[:rows, :query_cols], s.held[at, :query_cols], 1, 1)
+        return carry
+
+    lax.fori_loop(0, s.total.shape[1] // TILE, column, 0)
+
+
 def scatter_phase(n, ring, tokens, gain, out, s):
     rows, width = tokens.shape
     half = rows // 2
     last = n // 2
+    split = width // 2
+    query_cols = s.query.shape[1]
     me = lax.axis_index("tp")
     place = ring_place(me, n)
 
@@ -261,6 +285,17 @@
             ring[direction],
         )
 
+    def far_sender(direction, side):
+        part = pl.ds(direction * half, half)
+        lanes = pl.ds(side * split, split)
+        return remote(
+            s.outgoing.at[direction, last - 1, part, lanes],
+            s.incoming.at[direction, last - 1, part, lanes],
+            s.scatter_send.at[direction, last - 1, side],
+            s.scatter_recv.at[direction, last - 1, side],
+            ring[direction],
+        )
+
     def partial_sums(owners):
         for i, owner in enumerate(owners):
             s.picked[i * rows : (i + 1) * rows] = s.grads[rows_at(owner, rows)]
@@ -273,22 +308,44 @@
 
         lax.fori_loop(0, width // TILE, column, 0)
 
+    def arrivals(direction, hop, chunk):
+        if hop < last:
+            sender(direction, hop, chunk).wait_recv()
+        else:
+            for side in range(2):
+                far_sender(direction, side).wait_recv()
+
     sends = []
-    for hop in range(last, 0, -1):
-        owners = [ring_device(place + hop, n)]
-        if hop < last:
-            owners.append(ring_device(place - hop, n))
-        partial_sums(owners)
+    s.picked[:rows] = s.grads[rows_at(ring_device(place + last, n), rows)]
+    for side in range(2):
+
+        def add_pairs(j, carry):
+            at = rows_at(j, TILE)
+            s.total[:rows, at] += dot(
+                s.picked[:rows, query_cols:], s.held[at, query_cols:], 1, 1
+            )
+            return carry
+
+        tiles = split // TILE
+        lax.fori_loop(side * tiles, (side + 1) * tiles, add_pairs, 0)
+        lanes = slice(side * split, (side + 1) * split)
+        for direction in range(2):
+            part = slice(direction * half, (direction + 1) * half)
+            s.outgoing[direction, last - 1, part, lanes] = s.total[part, lanes].astype(jnp.bfloat16)
+            sends.append(far_sender(direction, side))
+            sends[-1].start()
+    for hop in range(last - 1, 0, -1):
+        partial_sums([ring_device(place + hop, n), ring_device(place - hop, n)])
         for position in (1, 0):
             for direction in range(2):
                 order = chunks_of(direction, hop, last)
                 if position < len(order):
                     chunk = order[position]
-                    base = direction * rows if hop < last else 0
+                    base = direction * rows
                     part = slice(chunk * half, (chunk + 1) * half)
                     value = s.total[base + chunk * half : base + (chunk + 1) * half]
-                    if hop < last and chunk in chunks_of(direction, hop + 1, last):
-                        sender(direction, hop + 1, chunk).wait_recv()
+                    if chunk in chunks_of(direction, hop + 1, last):
+                        arrivals(direction, hop + 1, chunk)
                         value = value + s.incoming[direction, hop, part].astype(jnp.float32)
                     s.outgoing[direction, hop - 1, part] = value.astype(jnp.bfloat16)
                     sends.append(sender(direction, hop, chunk))
@@ -299,7 +356,7 @@
         value = s.total[part]
         for direction in range(2):
             if chunk in chunks_of(direction, 1, last):
-                sender(direction, 1, chunk).wait_recv()
+                arrivals(direction, 1, chunk)
                 value = value + s.incoming[direction, 0, part].astype(jnp.float32)
         values = tokens[part].astype(jnp.float32)
         scale = lax.rsqrt(jnp.mean(values * values, axis=1, keepdims=True) + EPS)
@@ -311,17 +368,20 @@
     return sends
 
 
-def kernel(names, n, seqs, tokens, gain, output_grad, wq, wk, wv, out, *scratch):
+def kernel(names, n, seqs, tokens, gain_ref, output_grad, wq, wk, wv, out, *scratch):
     s = types.SimpleNamespace(**dict(zip(names, scratch)))
+    gain = s.gain
     loads = load_weights((wq, wk, wv), s.held, s.load_sems)
     place = ring_place(lax.axis_index("tp"), n)
     block = lax.axis_index("seq")
     ring = [{"tp": ring_device(place + step, n)} for step in (1, -1)]
     onward = [{"seq": (block + step) % seqs} for step in (1, 2)]
     backward = [{"seq": (block + seqs - step) % seqs} for step in (1, 2)]
+    gain[...] = gain_ref[...].reshape(gain.shape)
     greet(ring + onward + backward)
     sends = gather_phase(n, ring, onward, tokens, gain, loads, s)
-    sends += attention_phase(backward, output_grad, s)
+    meanwhile = functools.partial(farthest_query_sums, n, tokens.shape[0], s)
+    sends += attention_phase(backward, output_grad, s, meanwhile)
     sends += scatter_phase(n, ring, tokens, gain, out, s)
     for copy in sends:
         copy.wait_send()
@@ -338,8 +398,9 @@
     low, full = jnp.bfloat16, jnp.float32
     hops = pltpu.SemaphoreType.DMA((2, n // 2, 2))
     blocks = pltpu.SemaphoreType.DMA((2, n))
-    heads = pltpu.SemaphoreType.DMA((kv_heads, 2))
+    heads = pltpu.SemaphoreType.DMA((kv_heads, 3))
     scratch = dict(
+        gain=pltpu.VMEM((1, width), full),
         gathered=pltpu.VMEM((n, rows, width), low),
         held=pltpu.VMEM((width, cols), low),
         normed=pltpu.VMEM((2 * rows, width), low),
@@ -376,7 +437,7 @@
             collective_id=0, has_side_effects=True, vmem_limit_bytes=VMEM_BYTES
         ),
         name="attention_backward",
-    )(tokens, norm_gain.reshape(1, width), output_grad, query_weight, key_matrix, value_matrix)
+    )(tokens, norm_gain, output_grad, query_weight, key_matrix, value_matrix)
 
 
 def solution(mesh):

time: 129 us -> 125 us (0.969)
  Pallas kernels: 125 us -> 122 us
  local copies, waits for them, and re-layouts: 3.26 us -> 1.92 us
    pallas_call x1, Pallas kernels: 125 us -> 122 us  [on_device(): pl.pallas_call(functools.partial(kernel, tuple(scratch), n, lax.axis_size...]
    reshape x1 -> x0, local copies, waits for them, and re-layouts: 1.35 us -> none  [on_device(): norm_gain.reshape(1, width)]
where the time goes in v3:
time: 125 us; the launch traced here: 124 us
  Pallas kernels  122 us (98%)
  local copies, waits for them, and re-layouts  1.92 us (2%)
    pallas_call x1, Pallas kernels, on_device(): pl.pallas_call(functools.partial(kernel, tuple(scratch), n, lax.axis_size...  122 us

profile of v3, /device:TPU:0, one launch (start us, length us, event | category | flops | bytes accessed | tf_op | source)
XLA Modules:
  0.0 124.4 jit_solution(18394170089663336812)
XLA Ops:
  0.0 122.4 %attention_backward.1 = bf16[64,4608]{1,0:T(8,128)(2,1)} custom-call(bf16[64,4608]{1,0:T(8,128)(2,1)} %tokens.1, f32[4608]{0:T(1024)} %gain_ref.1, bf16[512,512]{1,0:T(8,128)(2,1)} %output_grad.1, bf16[4608,512]{1,0:T(8,128)(2,1)} %wq.1, bf16[4608,256]{1,0:T(8,128)(2,1)} %wk.1, bf16[4608,256]{1,0:T(8,128)(2,1)} %wv.1), custom_call_target="tpu_custom_call" | custom-call | tf_op jit(solution)/shard_map/attention_backward/pallas_call | solution.py:430
  122.4 1.9 %copy.8 = bf16[64,4608]{1,0:T(8,128)(2,1)} copy(bf16[64,4608]{1,0:T(8,128)(2,1)} %attention_backward.1) | data formatting | bytes 1179648
